TPU v7x, 32 devices: a whole 2x2x4 slice. The times are simulated.
32 devices in a mesh: seq: 8 (over y, x, core), batch: 4 (over z).
Axes of the slice: x: 2, y: 2, z: 4, core: 2. Of those that a mesh axis runs over, the one named last changes fastest.
Arguments:
- query_rows: bfloat16 [4, 1024, 2048], P('batch', 'seq'), may hold values from -6 to 6, as said below
- key_rows: bfloat16 [4, 1024, 1024], P('batch', 'seq'), may hold values from -6 to 6, as said below
- value_rows: bfloat16 [4, 1024, 1024], P('batch', 'seq'), may hold values from -6 to 6, as said below
- attn_output: bfloat16 [4, 1024, 2048], P('batch', 'seq'), may hold values from -6 to 6, as said below
- output_grad: bfloat16 [4, 1024, 2048], P('batch', 'seq'), may hold values from -6 to 6
- log_norm: float32 [4, 16, 1024], P('batch', None, 'seq'), as said below
- slab_order: int32 [4, 8], P('batch', 'seq'), may hold values from 0 to 7, as said below
- normed_input: bfloat16 [4, 1024, 4608], P('batch', 'seq'), may hold values from -6 to 6
Outputs:
- grad_query: bfloat16 [4, 1024, 2048], P('batch', 'seq')
- grad_key: bfloat16 [4, 1024, 1024], P('batch', 'seq')
- grad_weight: float32 [4608, 1024], P('seq')
Inputs may be any that keep to these rules, and one draw needn't show every extreme that they name: `query_rows`: queries of a causal forward pass with 16 heads. `key_rows`: keys of the same forward pass with 8 heads. `value_rows`: values of the same forward pass. `attn_output`: the forward pass's output: for each head, sum over keys at or before the query's position of exp(score - log_norm) times the value. `log_norm`: log of the sum of exp(score) over the keys at or before the query's position, so that each row's weights sum to one. `slab_order`: each row is a permutation of the slab places.
All inputs are finite; a program needn't handle non-finite values.
Results may differ from a plain program's by a relative error of at most 0.025.
Values may be sent and summed in bfloat16 or wider, within the bound.
A program may use at most 128 MiB of HBM per device.

v0:
```python
import jax
import jax.numpy as jnp
from jax import lax
from jax.sharding import PartitionSpec as P

HEADS = 16
KV_HEADS = 8
HEAD = 128
SCALE = 144.0 ** (-0.5)


def block_terms(queries, grads, delta, norms, query_pos, key_block, value_block, key_pos):
    keys_count = key_block.shape[0]
    scores = SCALE * jnp.einsum(
        "tgrd,kgd->grtk", queries, key_block, preferred_element_type=jnp.float32
    )
    allowed = key_pos[None, :] <= query_pos[:, None]
    probs = jnp.where(allowed, jnp.exp(scores - norms[..., None]), 0.0)
    dprob = jnp.einsum("tgrd,kgd->grtk", grads, value_block, preferred_element_type=jnp.float32)
    dscore = probs * (dprob - delta[..., None])
    probs_low = probs.astype(jnp.bfloat16)
    dscore_low = dscore.astype(jnp.bfloat16)
    grad_q = SCALE * jnp.einsum(
        "grtk,kgd->tgrd", dscore_low, key_block, preferred_element_type=jnp.float32
    )
    grad_k = SCALE * jnp.einsum(
        "grtk,tgrd->kgd", dscore_low, queries, preferred_element_type=jnp.float32
    )
    grad_v = jnp.einsum("grtk,tgrd->kgd", probs_low, grads, preferred_element_type=jnp.float32)
    return (grad_q, grad_k.reshape(keys_count, -1), grad_v.reshape(keys_count, -1))


def local(
    query_rows, key_rows, value_rows, attn_output, output_grad, log_norm, slab_order, normed_input
):
    tokens = query_rows.shape[1]
    group = HEADS // KV_HEADS
    kv_width = KV_HEADS * HEAD
    slabs = lax.axis_size("seq")
    length = tokens * slabs
    orders = lax.all_gather(slab_order, "seq", axis=1, tiled=True)
    queries = query_rows[0].reshape(tokens, KV_HEADS, group, HEAD)
    grads = output_grad[0].reshape(tokens, KV_HEADS, group, HEAD)
    outputs = attn_output[0].reshape(tokens, KV_HEADS, group, HEAD)
    delta = jnp.transpose(
        jnp.sum(grads.astype(jnp.float32) * outputs.astype(jnp.float32), axis=3), (1, 2, 0)
    )
    norms = log_norm[0].reshape(KV_HEADS, group, tokens)
    offsets = jnp.arange(tokens, dtype=jnp.int32)
    query_pos = slab_order[0, 0] * tokens + offsets
    width = tokens * -(-512 // tokens)
    empty_kv = jnp.zeros((length, kv_width), jnp.float32)
    empty_q = jnp.zeros((tokens, KV_HEADS, group, HEAD), jnp.float32)
    start = jnp.int32(0)
    grad_q = empty_q
    grad_k = empty_kv
    grad_v = empty_kv
    key_part = lax.all_gather(key_rows, "seq", axis=1, tiled=True)
    value_part = lax.all_gather(value_rows, "seq", axis=1, tiled=True)
    count = key_part.shape[1]
    for begin in range(0, count, width):
        finish = min(begin + width, count)
        shards = (finish - begin) // tokens
        first = (start + begin) // tokens
        places = lax.dynamic_slice_in_dim(orders[0], first, shards, 0)
        key_pos = (places[:, None] * tokens + offsets[None, :]).reshape(-1)
        key_block = key_part[0, begin:finish].reshape(-1, KV_HEADS, HEAD)
        value_block = value_part[0, begin:finish].reshape(-1, KV_HEADS, HEAD)
        term_q, term_k, term_v = block_terms(
            queries, grads, delta, norms, query_pos, key_block, value_block, key_pos
        )
        grad_q = grad_q + term_q
        grad_k = lax.dynamic_update_slice_in_dim(grad_k, term_k, begin, 0)
        grad_v = lax.dynamic_update_slice_in_dim(grad_v, term_v, begin, 0)
    grad_q, part_key, part_value = (grad_q, grad_k, grad_v)
    key_sum, value_sum = (
        lax.psum_scatter(
            part_key.astype(jnp.bfloat16), "seq", scatter_dimension=0, tiled=True
        ).astype(jnp.float32),
        lax.psum_scatter(
            part_value.astype(jnp.bfloat16), "seq", scatter_dimension=0, tiled=True
        ).astype(jnp.float32),
    )
    every_grad = lax.all_gather(value_sum.astype(jnp.bfloat16), "seq", axis=0, tiled=True)
    own_columns = lax.all_to_all(normed_input[0], "seq", split_axis=1, concat_axis=0, tiled=True)
    share = own_columns.shape[1]
    slab_parts = jnp.einsum(
        "std,stk->sdk",
        own_columns.reshape(slabs, tokens, share),
        every_grad.reshape(slabs, tokens, kv_width),
        preferred_element_type=jnp.float32,
    )
    rows_total = jnp.sum(slab_parts.astype(jnp.bfloat16).astype(jnp.float32), axis=0)
    weight = lax.psum(rows_total.astype(jnp.bfloat16), "batch").astype(jnp.float32)
    grad_query = grad_q.astype(jnp.bfloat16).reshape(1, tokens, HEADS * HEAD)
    grad_key = key_sum.astype(jnp.bfloat16).reshape(1, tokens, kv_width)
    return (grad_query, grad_key, weight)


def solution(mesh):
    placed = (
        P("batch", "seq", None),
        P("batch", "seq", None),
        P("batch", "seq", None),
        P("batch", "seq", None),
        P("batch", "seq", None),
        P("batch", None, "seq"),
        P("batch", "seq"),
        P("batch", "seq", None),
    )
    return jax.shard_map(
        local,
        mesh=mesh,
        in_specs=placed,
        out_specs=(P("batch", "seq", None), P("batch", "seq", None), P("seq", None)),
        check_vma=False,
    )
```

profile of v0, /device:TPU:0, one launch (start us, length us, event | category | flops | bytes accessed | tf_op | source)
XLA Modules:
  0.0 277.6 jit_solution(16221604361421081299)
XLA Ops:
  7.2 1.8 copy.57
  11.7 9.5 %all-reduce = s32[8]{0:T(128)S(1)} all-reduce(s32[8]{0:T(128)S(1)} %bitcast_dynamic-update-slice_fusion), channel_id=1, replica_groups=mesh['seq'=8,'batch'=4] {'seq'}, use_global_device_ids=true, to_apply=%add | all-reduce | flops 8 | bytes 64
  24.5 16.8 %all-gather.4.cloned.1.call-done = bf16[1,1024,1024]{1,2,0:T(8,128)(2,1)} async-done(((bf16[1,128,1024]{1,2,0:T(8,128)(2,1)}), bf16[1,1024,1024]{1,2,0:T(8,128)(2,1)}) %all-gather.4.cloned.1.call-update) | async-done | bytes 2097168 | tf_op jit(solution)/shard_map/all_gather | solution.py:58
  49.6 4.0 %copy.107 = bf16[1024,1024]{1,0:T(8,128)(2,1)} copy(bf16[1024,1024]{0,1:T(8,128)(2,1)} %pad_maximum_fusion.1) | data formatting | bytes 4194304
  54.6 40.3 %reduce-scatter.7.cloned.1.call-done = bf16[128,1024]{1,0:T(8,128)(2,1)} async-done(((bf16[1024,1024]{1,0:T(8,128)(2,1)}), bf16[128,1024]{1,0:T(8,128)(2,1)}) %reduce-scatter.7.cloned.1.call-update) | async-done | bytes 262160
  96.7 2.4 copy.81
  99.1 4.3 %all-to-all-start = ((bf16[128,8,576]{0,2,1:T(8,128)(2,1)}), bf16[128,8,576]{0,2,1:T(8,128)(2,1)}, u32[]{:S(2)}, u32[]{:S(2)}) async-start(bf16[128,8,576]{0,2,1:T(8,128)(2,1)} %bitcast.146), calls=%async_computation.1 | async-start | bytes 2359296 | tf_op jit(solution)/shard_map/all_to_all | solution.py:85
  103.5 3.1 %reshape.104 = f32[128,8,2,128]{3,2,1,0:T(2,128)} reshape(bf16[1,128,2048]{2,1,0:T(8,128)(2,1)} %param.11) | data formatting | bytes 1572864 | tf_op jit(solution)/shard_map/convert_element_type | solution.py:46
  106.6 3.2 %multiply_reduce_fusion = f32[128,8,2]{2,1,0:T(8,128)} fusion(f32[128,8,2,128]{3,2,1,0:T(2,128)} %reshape.104, bf16[128,8,2,128]{3,2,1,0:T(2,128)(2,1)S(1)} %reshape_squeeze.22), kind=kLoop, calls=%fused_computation.37 | loop fusion | flops 784384 | bytes 1581056 | tf_op jit(solution)/shard_map/reduce_sum | solution.py:46
  111.1 19.6 %all-gather.6.cloned.1.call-done = bf16[1,1024,1024]{1,2,0:T(8,128)(2,1)} async-done(((bf16[1,128,1024]{1,2,0:T(8,128)(2,1)}), bf16[1,1024,1024]{1,2,0:T(8,128)(2,1)}) %all-gather.6.cloned.1.call-update) | async-done | bytes 2097168 | tf_op jit(solution)/shard_map/all_gather | solution.py:59
  130.7 2.8 %fusion.35 = (bf16[1,512,1024]{1,2,0:T(8,128)(2,1)S(1)}, bf16[1,512,1024]{1,2,0:T(8,128)(2,1)}) fusion(bf16[1,1024,1024]{1,2,0:T(8,128)(2,1)} %all-gather.6.cloned.1.call-done), kind=kLoop, calls=%fused_computation.50 | loop fusion | bytes 4194304 | tf_op jit(solution)/shard_map/slice | solution.py:68
  133.6 2.9 %fusion.1 = bf16[8,2,128,512]{2,3,1,0:T(8,128)(2,1)} fusion(f32[8,512,128,2]{2,1,3,0:T(8,128)S(1)} %copy-done.4, bf16[512,8,128,1]{0,2,3,1:T(8,128)(2,1)S(1)} %bitcast.154, bf16[128,8,2,128]{0,3,2,1:T(8,128)(2,1)S(1)} %copy-done.7, f32[8,2,128]{2,1,0:T(2,128)S(1)} %copy.63, f32[8,2,128]{2,1,0:T(2,128)S(1)} %bitcast.161, ...), kind=kOutput, calls=%fused_computation.3 | convolution fusion | flops 274726912 | bytes 7946240 | tf_op jit(solution)/shard_map/tgrd,kgd->grtk/dot_general | solution.py:19
  136.5 24.1 %all-gather.8.cloned.1.call-done = bf16[1024,1024]{0,1:T(8,128)(2,1)} async-done(((bf16[128,1024]{0,1:T(8,128)(2,1)}), bf16[1024,1024]{0,1:T(8,128)(2,1)}) %all-gather.8.cloned.1.call-update) | async-done | bytes 2097168 | tf_op jit(solution)/shard_map/all_gather | solution.py:84
  160.6 3.9 %copy.80 = bf16[1024,1024]{1,0:T(8,128)(2,1)} copy(bf16[1024,1024]{0,1:T(8,128)(2,1)} %all-gather.8.cloned.1.call-done) | data formatting | bytes 4194304 | tf_op jit(solution)/shard_map/all_gather | solution.py:84
  164.5 5.8 %convert_reduce_fusion = bf16[1024,576]{0,1:T(8,128)(2,1)} fusion(bf16[8,128,1024]{2,1,0:T(8,128)(2,1)} %bitcast.150, bf16[128,8,576]{0,2,1:T(8,128)(2,1)} %all-to-all-done), kind=kOutput, calls=%fused_computation | convolution fusion | flops 1216806912 | bytes 4456448 | tf_op jit(solution)/shard_map/std,stk->sdk/dot_general | solution.py:87
  170.4 3.4 %fusion.14 = bf16[8,512,128]{1,2,0:T(8,128)(2,1)} fusion(bf16[8,2,128,512]{2,3,1,0:T(8,128)(2,1)} %fusion.1, bf16[128,8,2,128]{0,3,2,1:T(8,128)(2,1)S(1)} %bitcast.140), kind=kOutput, calls=%fused_computation.22 | convolution fusion | flops 269484032 | bytes 3670016 | tf_op jit(solution)/shard_map/grtk,tgrd->kgd/dot_general | solution.py:26
  173.8 2.3 copy.75
  176.1 4.0 %fusion.5 = bf16[8,2,128,512]{2,3,1,0:T(8,128)(2,1)S(1)} fusion(f32[8,512,128,2]{2,1,3,0:T(8,128)} %copy-done.2, bf16[512,8,128,1]{0,2,3,1:T(8,128)(2,1)} %bitcast.153, bf16[128,8,2,128]{0,3,2,1:T(8,128)(2,1)S(1)} %copy-done.7, f32[8,2,128]{2,1,0:T(2,128)S(1)} %copy.63, f32[8,2,128]{2,1,0:T(2,128)S(1)} %bitcast.162, pred[128,512]{0,1:T(8,128)(4,1)S(1)} %get-tuple-element.17), kind=kOutput, calls=%fused_computation.9 | convolution fusion | flops 274726912 | bytes 7946240 | tf_op jit(solution)/shard_map/tgrd,kgd->grtk/dot_general | solution.py:19
  181.9 2.3 copy.74
  184.2 3.1 %pad_maximum_fusion = bf16[1024,1024]{1,0:T(8,128)(2,1)} fusion(bf16[512,1024]{1,0:T(8,128)(2,1)} %copy.75, bf16[512,1024]{1,0:T(8,128)(2,1)} %copy.74), kind=kLoop, calls=%fused_computation.17 | loop fusion | flops 4194304 | bytes 4194304 | tf_op jit(solution)/shard_map/dynamic_update_slice | solution.py:73
  187.3 2.3 fusion.39
  191.1 35.4 %all-reduce.3.cloned.1.call-done = bf16[576,1024]{1,0:T(8,128)(2,1)} async-done(((bf16[576,1024]{1,0:T(8,128)(2,1)}), bf16[576,1024]{1,0:T(8,128)(2,1)}) %all-reduce.3.cloned.1.call-update) | async-done | bytes 1179664 | tf_op jit(solution)/shard_map/psum | solution.py:94
  226.5 3.0 %convert_element_type.60 = f32[576,1024]{1,0:T(8,128)} convert(bf16[576,1024]{1,0:T(8,128)(2,1)} %all-reduce.3.cloned.1.call-done) | non-fusion elementwise | flops 589824 | bytes 3538944 | tf_op jit(solution)/shard_map/convert_element_type | solution.py:94
  229.5 41.3 %reduce-scatter.5.cloned.1.call-done = bf16[128,1024]{1,0:T(8,128)(2,1)} async-done(((bf16[1024,1024]{1,0:T(8,128)(2,1)}), bf16[128,1024]{1,0:T(8,128)(2,1)}) %reduce-scatter.5.cloned.1.call-update) | async-done | bytes 262160 | tf_op jit(solution)/shard_map/reduce_scatter | solution.py:77
  (55 shorter events, 21.3 us)
Async XLA Ops:
  7.2 16.6 %copy-start.5 = (bf16[1,128,2048]{2,1,0:T(8,128)(2,1)S(1)}, bf16[1,128,2048]{2,1,0:T(8,128)(2,1)}, u32[]{:S(2)}) copy-start(bf16[1,128,2048]{2,1,0:T(8,128)(2,1)} %param.8) | copy-start | bytes 1572868
  7.2 34.1 %all-gather.4.cloned.1.call-start = ((), (), s32[]{:S(2)}) async-start(), calls=%async_computation.3 | async-start | bytes 2359296 | tf_op jit(solution)/shard_map/all_gather | solution.py:58
  9.1 85.8 %reduce-scatter.7.cloned.1.call-start = ((), (), s32[]{:S(2)}) async-start(), calls=%async_computation.8 | async-start | bytes 2359296
  43.7 2.0 copy-start.3
  43.8 2.0 copy-start.6
  43.8 2.0 copy-start.9
  44.5 2.4 copy-start.2
  49.6 4.1 %copy-start.8 = (bf16[1,128,1024]{2,1,0:T(8,128)(2,1)S(1)}, bf16[1,128,1024]{2,1,0:T(8,128)(2,1)}, u32[]{:S(2)}) copy-start(bf16[1,128,1024]{2,1,0:T(8,128)(2,1)} %param.10) | copy-start | bytes 786436
  53.6 77.1 %all-gather.6.cloned.1.call-start = ((), (), s32[]{:S(2)}) async-start(), calls=%async_computation.4 | async-start | bytes 2359296 | tf_op jit(solution)/shard_map/all_gather | solution.py:59
  54.5 106.0 %all-gather.8.cloned.1.call-start = ((), (), s32[]{:S(2)}) async-start(), calls=%async_computation.6 | async-start | bytes 2359296 | tf_op jit(solution)/shard_map/all_gather | solution.py:84
  99.1 65.4 %all-to-all-start = ((bf16[128,8,576]{0,2,1:T(8,128)(2,1)}), bf16[128,8,576]{0,2,1:T(8,128)(2,1)}, u32[]{:S(2)}, u32[]{:S(2)}) async-start(bf16[128,8,576]{0,2,1:T(8,128)(2,1)} %bitcast.146), calls=%async_computation.1 | async-start | bytes 2359296 | tf_op jit(solution)/shard_map/all_to_all | solution.py:85
  103.3 123.2 %all-reduce.3.cloned.1.call-start = ((), (), s32[]{:S(2)}) async-start(), calls=%async_computation.7 | async-start | bytes 2359296 | tf_op jit(solution)/shard_map/psum | solution.py:94
  109.9 23.7 %copy-start.7 = (bf16[128,8,2,128]{0,3,2,1:T(8,128)(2,1)S(1)}, bf16[128,8,2,128]{0,3,2,1:T(8,128)(2,1)}, u32[]{:S(2)}) copy-start(bf16[128,8,2,128]{0,3,2,1:T(8,128)(2,1)} %copy.77) | copy-start | bytes 1572868
  130.7 2.9 %copy-start.4 = (f32[8,512,128,2]{2,1,3,0:T(8,128)S(1)}, f32[8,512,128,2]{2,1,3,0:T(8,128)}, u32[]{:S(2)}) copy-start(f32[8,512,128,2]{2,1,3,0:T(8,128)} %copy-done.3) | copy-start | bytes 12582916
  170.4 100.4 %reduce-scatter.5.cloned.1.call-start = ((), (), s32[]{:S(2)}) async-start(), calls=%async_computation.5 | async-start | bytes 2359296 | tf_op jit(solution)/shard_map/reduce_scatter | solution.py:77
  180.0 1.8 copy-start.1
  187.3 2.3 copy-start
Sparse Core Ops, SparseCore 0:
  10.4 30.8 all-gather.3
  53.7 41.0 reduce-scatter.6
  97.3 33.3 all-gather.5
  132.4 28.0 all-gather.7
  170.5 55.9 all-reduce.2
  230.2 40.5 reduce-scatter.4
where the time goes:
time: 278 us
  waiting for transfers between devices  178 us (64%)
  local copies, waits for them, and re-layouts  35.5 us (13%)
  matrix products  24.2 us (9%)
  between operations  14.9 us (5%)
  other arithmetic  11.3 us (4%)
  blocking collectives  9.51 us (3%)
  starting transfers between devices  4.68 us (2%)
    reduce_scatter x1, waiting for transfers between devices, local(): lax.psum_scatter(part_key.astype(jnp.bfloat16), 'seq', scatter_dimension=...  41.3 us
    unnamed x7, waiting for transfers between devices  40.4 us
    psum x1, waiting for transfers between devices, local(): lax.psum(rows_total.astype(jnp.bfloat16), 'batch').astype(jnp.float32)  35.4 us
    all_gather x1, waiting for transfers between devices, local(): lax.all_gather(value_sum.astype(jnp.bfloat16), 'seq', axis=0, tiled=True)  24.1 us
    all_gather x1, waiting for transfers between devices, local(): value_part = lax.all_gather(value_rows, 'seq', axis=1, tiled=True)  19.6 us
    all_gather x1, waiting for transfers between devices, local(): key_part = lax.all_gather(key_rows, 'seq', axis=1, tiled=True)  16.8 us
    unnamed x29, local copies, waits for them, and re-layouts  15.3 us
    unnamed x1, blocking collectives  9.51 us
  transfers between devices with their start and end apart: 7, of which 6 were waited for; matrix products, arithmetic and copies ran while one was open for 18% of the time, Pallas kernels for 0%

commit v1 on v0

--- a/solution.py
+++ b/solution.py
@@ -56,7 +56,7 @@
     grad_k = empty_kv
     grad_v = empty_kv
     key_part = lax.all_gather(key_rows, "seq", axis=1, tiled=True)
-    value_part = lax.all_gather(value_rows, "seq", axis=1, tiled=True)
+    value_part = jnp.concatenate(lax.all_gather(value_rows, "seq"), axis=1)
     count = key_part.shape[1]
     for begin in range(0, count, width):
         finish = min(begin + width, count)

time: 278 us -> 279 us (level)
  waiting for transfers between devices: 178 us -> 171 us
  local copies, waits for them, and re-layouts: 35.5 us -> 39.3 us
    all_gather x1, waiting for transfers between devices: 24.1 us -> 17.3 us  [local(): lax.all_gather(value_sum.astype(jnp.bfloat16), 'seq', axis=0, tiled=True)]
    unnamed x29 -> x26, local copies, waits for them, and re-layouts: 15.3 us -> 18.9 us
  transfers between devices with their start and end apart: 7 -> 7, of which waited for: 6 -> 6; matrix products, arithmetic and copies ran while one was open for 18% -> 21% of each run, Pallas kernels for 0% -> 0%
where the time goes in v1:
time: 279 us; the launch traced here: 278 us
  waiting for transfers between devices  171 us (61%)
  local copies, waits for them, and re-layouts  39.3 us (14%)
  matrix products  26.8 us (10%)
  between operations  14.9 us (5%)
  other arithmetic  11.3 us (4%)
  blocking collectives  9.51 us (3%)
  starting transfers between devices  4.68 us (2%)
    reduce_scatter x1, waiting for transfers between devices, local(): lax.psum_scatter(part_key.astype(jnp.bfloat16), 'seq', scatter_dimension=...  41.3 us
    unnamed x7, waiting for transfers between devices  41.2 us
    psum x1, waiting for transfers between devices, local(): lax.psum(rows_total.astype(jnp.bfloat16), 'batch').astype(jnp.float32)  35.4 us
    all_gather x1, waiting for transfers between devices, local(): value_part = jnp.concatenate(lax.all_gather(value_rows, 'seq'), axis=1)  19.1 us
    unnamed x26, local copies, waits for them, and re-layouts  18.9 us
    all_gather x1, waiting for transfers between devices, local(): lax.all_gather(value_sum.astype(jnp.bfloat16), 'seq', axis=0, tiled=True)  17.3 us
    all_gather x1, waiting for transfers between devices, local(): key_part = lax.all_gather(key_rows, 'seq', axis=1, tiled=True)  16.8 us
    unnamed x1, blocking collectives  9.51 us
  transfers between devices with their start and end apart: 7, of which 6 were waited for; matrix products, arithmetic and copies ran while one was open for 21% of the time, Pallas kernels for 0%

profile of v1, /device:TPU:0, one launch (start us, length us, event | category | flops | bytes accessed | tf_op | source)
XLA Modules:
  0.0 277.6 jit_solution(2072631305019797407)
XLA Ops:
  11.7 9.5 %all-reduce = s32[8]{0:T(128)S(1)} all-reduce(s32[8]{0:T(128)S(1)} %bitcast_dynamic-update-slice_fusion), channel_id=1, replica_groups=mesh['seq'=8,'batch'=4] {'seq'}, use_global_device_ids=true, to_apply=%add | all-reduce | flops 8 | bytes 64
  24.5 16.8 %all-gather.5.cloned.1.call-done = bf16[1,1024,1024]{1,2,0:T(8,128)(2,1)} async-done(((bf16[1,128,1024]{1,2,0:T(8,128)(2,1)}), bf16[1,1024,1024]{1,2,0:T(8,128)(2,1)}) %all-gather.5.cloned.1.call-update) | async-done | bytes 2097168 | tf_op jit(solution)/shard_map/all_gather | solution.py:58
  49.6 3.9 %copy.108 = bf16[1024,1024]{1,0:T(8,128)(2,1)} copy(bf16[1024,1024]{0,1:T(8,128)(2,1)} %pad_maximum_fusion.1) | data formatting | bytes 4194304
  54.3 40.5 %reduce-scatter.7.cloned.1.call-done = bf16[128,1024]{1,0:T(8,128)(2,1)} async-done(((bf16[1024,1024]{1,0:T(8,128)(2,1)}), bf16[128,1024]{1,0:T(8,128)(2,1)}) %reduce-scatter.7.cloned.1.call-update) | async-done | bytes 262160
  96.6 2.4 copy.81
  99.0 4.3 %all-to-all-start = ((bf16[128,8,576]{0,2,1:T(8,128)(2,1)}), bf16[128,8,576]{0,2,1:T(8,128)(2,1)}, u32[]{:S(2)}, u32[]{:S(2)}) async-start(bf16[128,8,576]{0,2,1:T(8,128)(2,1)} %bitcast.147), calls=%async_computation.1 | async-start | bytes 2359296 | tf_op jit(solution)/shard_map/all_to_all | solution.py:85
  103.5 3.1 %reshape.108 = f32[128,8,2,128]{3,2,1,0:T(2,128)} reshape(bf16[1,128,2048]{2,1,0:T(8,128)(2,1)} %param.11) | data formatting | bytes 1572864 | tf_op jit(solution)/shard_map/convert_element_type | solution.py:46
  106.6 3.2 %multiply_reduce_fusion = f32[128,8,2]{2,1,0:T(8,128)} fusion(f32[128,8,2,128]{3,2,1,0:T(2,128)} %reshape.108, bf16[128,8,2,128]{3,2,1,0:T(2,128)(2,1)S(1)} %reshape_squeeze.22), kind=kLoop, calls=%fused_computation.37 | loop fusion | flops 784384 | bytes 1581056 | tf_op jit(solution)/shard_map/reduce_sum | solution.py:46
  111.0 19.1 %all-gather.9.cloned.1.call-done = bf16[8,128,1024]{2,1,0:T(8,128)(2,1)} async-done(((bf16[1,128,1024]{2,1,0:T(8,128)(2,1)}), bf16[8,128,1024]{2,1,0:T(8,128)(2,1)}) %all-gather.9.cloned.1.call-update) | async-done | bytes 2097168 | tf_op jit(solution)/shard_map/all_gather | solution.py:59
  130.1 3.0 %fusion.35 = (bf16[1,512,1024]{2,1,0:T(8,128)(2,1)}, bf16[1,512,1024]{2,1,0:T(8,128)(2,1)}) fusion(bf16[1,1024,1024]{2,1,0:T(8,128)(2,1)} %bitcast.151), kind=kLoop, calls=%fused_computation.50 | loop fusion | bytes 4194304 | tf_op jit(solution)/shard_map/slice | solution.py:68
  133.2 2.3 copy.111
  135.5 2.3 copy.110
  137.8 5.5 %fusion.1 = bf16[8,2,128,512]{2,3,1,0:T(8,128)(2,1)} fusion(f32[8,512,128,2]{2,1,3,0:T(8,128)} %copy-done.3, bf16[512,8,128,1]{0,2,3,1:T(8,128)(2,1)} %bitcast.156, bf16[128,8,2,128]{0,3,2,1:T(8,128)(2,1)S(1)} %copy-done.6, f32[8,2,128]{2,1,0:T(2,128)S(1)} %copy.63, f32[8,2,128]{2,1,0:T(2,128)S(1)} %bitcast.163, pred[128,512]{0,1:T(8,128)(4,1)S(1)} %get-tuple-element.16), kind=kOutput, calls=%fused_computation.3 | convolution fusion | flops 274726912 | bytes 7946240 | tf_op jit(solution)/shard_map/tgrd,kgd->grtk/dot_general | solution.py:19
  143.3 17.3 %all-gather.7.cloned.1.call-done = bf16[1024,1024]{0,1:T(8,128)(2,1)} async-done(((bf16[128,1024]{0,1:T(8,128)(2,1)}), bf16[1024,1024]{0,1:T(8,128)(2,1)}) %all-gather.7.cloned.1.call-update) | async-done | bytes 2097168 | tf_op jit(solution)/shard_map/all_gather | solution.py:84
  160.6 3.9 %copy.80 = bf16[1024,1024]{1,0:T(8,128)(2,1)} copy(bf16[1024,1024]{0,1:T(8,128)(2,1)} %all-gather.7.cloned.1.call-done) | data formatting | bytes 4194304 | tf_op jit(solution)/shard_map/all_gather | solution.py:84
  164.5 5.9 %convert_reduce_fusion = bf16[1024,576]{0,1:T(8,128)(2,1)} fusion(bf16[8,128,1024]{2,1,0:T(8,128)(2,1)} %bitcast.152, bf16[128,8,576]{0,2,1:T(8,128)(2,1)} %all-to-all-done), kind=kOutput, calls=%fused_computation | convolution fusion | flops 1216806912 | bytes 4456448 | tf_op jit(solution)/shard_map/std,stk->sdk/dot_general | solution.py:87
  170.4 3.4 %fusion.14 = bf16[8,512,128]{1,2,0:T(8,128)(2,1)} fusion(bf16[8,2,128,512]{2,3,1,0:T(8,128)(2,1)} %fusion.1, bf16[128,8,2,128]{0,3,2,1:T(8,128)(2,1)S(1)} %bitcast.141), kind=kOutput, calls=%fused_computation.22 | convolution fusion | flops 269484032 | bytes 3670016 | tf_op jit(solution)/shard_map/grtk,tgrd->kgd/dot_general | solution.py:26
  173.8 2.3 copy.75
  176.1 4.0 %fusion.5 = bf16[8,2,128,512]{2,3,1,0:T(8,128)(2,1)S(1)} fusion(f32[8,512,128,2]{2,1,3,0:T(8,128)} %copy-done.2, bf16[512,8,128,1]{0,2,3,1:T(8,128)(2,1)} %bitcast.155, bf16[128,8,2,128]{0,3,2,1:T(8,128)(2,1)S(1)} %copy-done.6, f32[8,2,128]{2,1,0:T(2,128)S(1)} %copy.63, f32[8,2,128]{2,1,0:T(2,128)S(1)} %bitcast.164, pred[128,512]{0,1:T(8,128)(4,1)S(1)} %get-tuple-element.17), kind=kOutput, calls=%fused_computation.9 | convolution fusion | flops 274726912 | bytes 7946240 | tf_op jit(solution)/shard_map/tgrd,kgd->grtk/dot_general | solution.py:19
  181.9 2.3 copy.74
  184.1 3.1 %pad_maximum_fusion = bf16[1024,1024]{1,0:T(8,128)(2,1)} fusion(bf16[512,1024]{1,0:T(8,128)(2,1)} %copy.75, bf16[512,1024]{1,0:T(8,128)(2,1)} %copy.74), kind=kLoop, calls=%fused_computation.17 | loop fusion | flops 4194304 | bytes 4194304 | tf_op jit(solution)/shard_map/dynamic_update_slice | solution.py:73
  191.1 35.4 %all-reduce.3.cloned.1.call-done = bf16[576,1024]{1,0:T(8,128)(2,1)} async-done(((bf16[576,1024]{1,0:T(8,128)(2,1)}), bf16[576,1024]{1,0:T(8,128)(2,1)}) %all-reduce.3.cloned.1.call-update) | async-done | bytes 1179664 | tf_op jit(solution)/shard_map/psum | solution.py:94
  226.5 3.0 %convert_element_type.60 = f32[576,1024]{1,0:T(8,128)} convert(bf16[576,1024]{1,0:T(8,128)(2,1)} %all-reduce.3.cloned.1.call-done) | non-fusion elementwise | flops 589824 | bytes 3538944 | tf_op jit(solution)/shard_map/convert_element_type | solution.py:94
  229.5 41.3 %reduce-scatter.5.cloned.1.call-done = bf16[128,1024]{1,0:T(8,128)(2,1)} async-done(((bf16[1024,1024]{1,0:T(8,128)(2,1)}), bf16[128,1024]{1,0:T(8,128)(2,1)}) %reduce-scatter.5.cloned.1.call-update) | async-done | bytes 262160 | tf_op jit(solution)/shard_map/reduce_scatter | solution.py:77
  (52 shorter events, 25.0 us)
Async XLA Ops:
  7.2 16.6 %copy-start.4 = (bf16[1,128,2048]{2,1,0:T(8,128)(2,1)S(1)}, bf16[1,128,2048]{2,1,0:T(8,128)(2,1)}, u32[]{:S(2)}) copy-start(bf16[1,128,2048]{2,1,0:T(8,128)(2,1)} %param.8) | copy-start | bytes 1572868
  7.2 34.1 %all-gather.5.cloned.1.call-start = ((), (), s32[]{:S(2)}) async-start(), calls=%async_computation.3 | async-start | bytes 2359296 | tf_op jit(solution)/shard_map/all_gather | solution.py:58
  9.1 85.7 %reduce-scatter.7.cloned.1.call-start = ((), (), s32[]{:S(2)}) async-start(), calls=%async_computation.8 | async-start | bytes 2359296
  43.7 2.0 copy-start.3
  43.8 2.0 copy-start.5
  43.8 1.9 copy-start.7
  44.5 2.4 copy-start.2
  53.5 76.6 %all-gather.9.cloned.1.call-start = ((), (), s32[]{:S(2)}) async-start(), calls=%async_computation.7 | async-start | bytes 2359296 | tf_op jit(solution)/shard_map/all_gather | solution.py:59
  54.3 106.3 %all-gather.7.cloned.1.call-start = ((), (), s32[]{:S(2)}) async-start(), calls=%async_computation.5 | async-start | bytes 2359296 | tf_op jit(solution)/shard_map/all_gather | solution.py:84
  99.0 65.5 %all-to-all-start = ((bf16[128,8,576]{0,2,1:T(8,128)(2,1)}), bf16[128,8,576]{0,2,1:T(8,128)(2,1)}, u32[]{:S(2)}, u32[]{:S(2)}) async-start(bf16[128,8,576]{0,2,1:T(8,128)(2,1)} %bitcast.147), calls=%async_computation.1 | async-start | bytes 2359296 | tf_op jit(solution)/shard_map/all_to_all | solution.py:85
  103.3 123.2 %all-reduce.3.cloned.1.call-start = ((), (), s32[]{:S(2)}) async-start(), calls=%async_computation.6 | async-start | bytes 2359296 | tf_op jit(solution)/shard_map/psum | solution.py:94
  133.2 4.6 %copy-start.6 = (bf16[128,8,2,128]{0,3,2,1:T(8,128)(2,1)S(1)}, bf16[128,8,2,128]{0,3,2,1:T(8,128)(2,1)}, u32[]{:S(2)}) copy-start(bf16[128,8,2,128]{0,3,2,1:T(8,128)(2,1)} %copy.77) | copy-start | bytes 1572868
  170.4 100.4 %reduce-scatter.5.cloned.1.call-start = ((), (), s32[]{:S(2)}) async-start(), calls=%async_computation.4 | async-start | bytes 2359296 | tf_op jit(solution)/shard_map/reduce_scatter | solution.py:77
  180.1 1.8 copy-start.1
  187.2 2.3 copy-start
Sparse Core Ops, SparseCore 0:
  10.4 30.8 all-gather.4
  53.7 41.0 reduce-scatter.6
  96.7 33.3 all-gather.8
  132.4 28.0 all-gather.6
  170.5 55.9 all-reduce.2
  230.2 40.5 reduce-scatter.4
